TPU v7x, 128 devices: a whole 4x4x4 slice. The times are simulated.
128 devices in a mesh: member: 16 (over z, x_lo, core), space: 8 (over x_hi, y).
Axes of the slice: x: 4 (x_hi: 2, x_lo: 2; x = x_hi * 2 + x_lo), y: 4, z: 4, core: 2. Of those that a mesh axis runs over, the one named last changes fastest.
Arguments:
- weather: bfloat16 [16, 84, 256, 1440], P('member', None, 'space'), may hold values from -6 to 6
- coefficients: int32 [16, 84, 2, 368, 361], P('member', None, None, 'space'), may hold values from -1073741824 to 1073741823
- channel_scale: float32 [84], replicated, may hold values from 0.3 to 3
Outputs:
- perturbed: bfloat16 [16, 84, 256, 1440], P('member', None, 'space')
All inputs are finite; a program needn't handle non-finite values.
Results may differ from a plain program's by a relative error of at most 0.007.
Values may be sent and summed in bfloat16 or wider, within the bound.
No kernel may reach another device: no remote copies, remote signals or barrier semaphores. Data moves between devices by JAX's collectives and lax.ppermute only.
A program may use at most 192 MiB of HBM per device.

v0:
```python
import math

import jax
import jax.numpy as jnp
from jax import lax
from jax.sharding import PartitionSpec as P


def in_blocks(array, dim, devices):
    lengths = array.shape
    parts = array.reshape(*lengths[:dim], devices, lengths[dim] // devices, *lengths[dim + 1 :])
    return jnp.moveaxis(parts, dim, 0)


def joined_along(parts, dim):
    lengths = list(parts.shape[1:])
    lengths[dim] *= parts.shape[0]
    return jnp.moveaxis(parts, 0, dim).reshape(lengths)


def exchange_both(array, axis, axes, splits, concats):
    sizes = [lax.axis_size(a) for a in axes]
    parts = in_blocks(array, splits[0], sizes[0])
    parts = jnp.moveaxis(in_blocks(parts, splits[1] + 1, sizes[1]), 0, 1)
    inside = parts.shape[2:]
    parts = parts.reshape(-1, *inside)
    parts = lax.all_to_all(parts, axis, split_axis=0, concat_axis=0, tiled=True)
    parts = joined_along(parts.reshape(*sizes, *inside), concats[0] + 1)
    return joined_along(parts, concats[1])


def diagonal_log(order_count):
    steps_up = jnp.arange(1, order_count, dtype=jnp.int32).astype(jnp.float32)
    terms = 0.5 * jnp.log((2.0 * steps_up + 1.0) / (2.0 * steps_up))
    return jnp.concatenate([jnp.zeros((1,), jnp.float32), jnp.cumsum(terms)])


def legendre_table(orders, colatitude, order_logs, degree_count):
    order_values = orders.astype(jnp.float32)[:, None]
    cosine = jnp.cos(colatitude)[None, :]
    sine_values = jnp.sin(colatitude)[None, :]
    diagonal = jnp.exp(
        order_logs[:, None] - 0.5 * math.log(4.0 * math.pi) + order_values * jnp.log(sine_values)
    )
    block_size = 16
    turn_count = (degree_count + block_size - 1) // block_size
    order_square = order_values * order_values

    def advance(carry, turn_index):
        older_row, newer_row = carry
        produced = []
        for inner_step in range(block_size):
            degree = (turn_index * block_size + inner_step).astype(jnp.float32)
            degree_square = degree * degree
            prior = degree - 1.0
            factor_up = jnp.sqrt(
                jnp.maximum(4.0 * degree_square - 1.0, 1.0)
                / jnp.maximum(degree_square - order_square, 1.0)
            )
            factor_down = jnp.sqrt(
                jnp.maximum(prior * prior - order_square, 0.0)
                / jnp.maximum(4.0 * prior * prior - 1.0, 1.0)
            )
            next_row = factor_up * (cosine * newer_row - factor_down * older_row)
            next_row = jnp.where(
                degree < order_values, 0.0, jnp.where(degree == order_values, diagonal, next_row)
            )
            produced.append(next_row)
            older_row, newer_row = (newer_row, next_row)
        return ((older_row, newer_row), jnp.stack(produced))

    empty = jnp.zeros_like(diagonal)
    carried, stacked = lax.scan(advance, (empty, empty), jnp.arange(turn_count, dtype=jnp.int32))
    return stacked.reshape(turn_count * block_size, orders.shape[0], colatitude.shape[0])[
        :degree_count
    ]


def spectral_values(coefficients, orders):
    degree_count = coefficients.shape[-1]
    degrees = jnp.arange(degree_count, dtype=jnp.int32)
    keep = degrees[None, :] >= orders[:, None]
    factor = math.sqrt(3.0) * math.sqrt(4.0 * math.pi) / degree_count * 2.0 ** (-30)
    values = coefficients.astype(jnp.float32) * factor
    return jnp.where(keep, values, 0.0).astype(jnp.bfloat16)


def fourier_basis(order_count, lon_count):
    orders = jnp.arange(order_count, dtype=jnp.int32)
    columns = jnp.arange(lon_count, dtype=jnp.int32)
    phases = orders[:, None] * columns[None, :] % lon_count
    angles = 2.0 * math.pi / lon_count * phases.astype(jnp.float32)
    weights = jnp.where(orders == 0, 1.0, math.sqrt(2.0)).astype(jnp.float32)[:, None]
    return jnp.stack([weights * jnp.cos(angles), weights * jnp.sin(angles)]).astype(jnp.bfloat16)


def local(weather, coefficients, channel_scale):
    group_count = lax.axis_size("member")
    band_count = lax.axis_size("space")
    member_local, channels, rows_local, lon_count = weather.shape
    order_local = coefficients.shape[3]
    degree_count = coefficients.shape[4]
    order_count = order_local * band_count
    lat_count = rows_local * band_count
    lat_local = rows_local // group_count
    member_count = member_local * group_count
    first_order = lax.axis_index("space") * order_local
    orders = first_order + jnp.arange(order_local, dtype=jnp.int32)
    order_logs = lax.dynamic_slice_in_dim(diagonal_log(order_count), first_order, order_local)
    row_first = (lon_count // 2 + 1 - lat_count) // 2
    colatitude = (
        math.pi
        * (row_first + jnp.arange(lat_count, dtype=jnp.int32)).astype(jnp.float32)
        / (lon_count // 2)
    )
    legendre = legendre_table(orders, colatitude, order_logs, degree_count).astype(jnp.bfloat16)
    spectral = spectral_values(coefficients, orders)
    fourier = jnp.einsum(
        "ecpml,lmt->ectpm", spectral, legendre, preferred_element_type=jnp.float32
    ).astype(jnp.bfloat16)
    fourier = fourier.reshape(
        member_local, channels, band_count, group_count, lat_local, 2, order_local
    )
    basis = fourier_basis(order_count, lon_count).reshape(2 * order_count, lon_count)
    scale_wide = channel_scale[None, :, None, None, None]
    pieces = weather.reshape(member_local, channels, group_count, lat_local, lon_count)
    banded = exchange_both(fourier, ("member", "space"), ("member", "space"), (3, 2), (0, 6))
    fourier_rows = banded.reshape(member_count * channels * lat_local, 2 * order_count)
    noise = jnp.dot(fourier_rows, basis, preferred_element_type=jnp.float32).astype(jnp.bfloat16)
    noise = noise.reshape(member_count, channels, 1, lat_local, lon_count)
    noise_wide = lax.optimization_barrier(noise).astype(jnp.float32)
    band_mean = jnp.sum(noise_wide, axis=0, keepdims=True) / member_count
    weather_bands = lax.all_to_all(pieces, "member", split_axis=2, concat_axis=0, tiled=True)
    perturbed = (weather_bands.astype(jnp.float32) + scale_wide * (noise_wide - band_mean)).astype(
        jnp.bfloat16
    )
    returned = lax.all_to_all(perturbed, "member", split_axis=0, concat_axis=2, tiled=True)
    return returned.reshape(member_local, channels, rows_local, lon_count)


def solution(mesh):
    return jax.shard_map(
        local,
        mesh=mesh,
        in_specs=(P("member", None, "space", None), P("member", None, None, "space", None), P()),
        out_specs=P("member", None, "space", None),
        check_vma=False,
    )
```

profile of v0, /device:TPU:1, one launch (start us, length us, event | category | flops | bytes accessed | tf_op | source)
XLA Modules:
  0.0 521.1 jit_solution(6489075889256272937)
XLA Ops:
  0.9 127.6 %while.21 = (s32[]{:T(128)}, f32[46,256]{1,0:T(8,128)S(1)}, f32[46,256]{1,0:T(8,128)S(1)}, bf16[23,16,46,256]{3,2,1,0:T(8,128)(2,1)}, s32[23]{0:T(128)S(1)}, /*i...) while((s32[]{:T(128)}, f32[46,256]{1,0:T(8,128)S(1)}, ...), condition=%wide.region_3.4_spmd.clone.clone.clone.clone, body=%wide.region_2.3_spmd.clone.clone.clone.clone.sunk | while | flops 3519778 | bytes 3859869 | solution.py:73
  0.9 0.6 dynamic_slice.18
  5.7 0.8 bitcast_dynamic-update-slice_fusion.50
  6.4 0.6 dynamic_slice.18
  11.2 0.8 bitcast_dynamic-update-slice_fusion.50
  16.7 0.8 bitcast_dynamic-update-slice_fusion.50
  22.3 0.8 bitcast_dynamic-update-slice_fusion.50
  27.8 0.8 bitcast_dynamic-update-slice_fusion.50
  33.3 0.8 bitcast_dynamic-update-slice_fusion.50
  38.9 0.8 bitcast_dynamic-update-slice_fusion.50
  44.4 0.8 bitcast_dynamic-update-slice_fusion.50
  50.0 0.8 bitcast_dynamic-update-slice_fusion.50
  55.5 0.8 bitcast_dynamic-update-slice_fusion.50
  61.0 0.8 bitcast_dynamic-update-slice_fusion.50
  66.6 0.8 bitcast_dynamic-update-slice_fusion.50
  72.1 0.8 bitcast_dynamic-update-slice_fusion.50
  77.7 0.8 bitcast_dynamic-update-slice_fusion.50
  83.2 0.8 bitcast_dynamic-update-slice_fusion.50
  88.7 0.8 bitcast_dynamic-update-slice_fusion.50
  94.3 0.8 bitcast_dynamic-update-slice_fusion.50
  99.8 0.8 bitcast_dynamic-update-slice_fusion.50
  105.4 0.8 bitcast_dynamic-update-slice_fusion.50
  110.9 0.8 bitcast_dynamic-update-slice_fusion.50
  116.5 0.8 bitcast_dynamic-update-slice_fusion.50
  122.1 0.8 bitcast_dynamic-update-slice_fusion.50
  127.7 0.8 bitcast_dynamic-update-slice_fusion.50
  128.5 10.1 %copy.39 = bf16[23,16,46,256]{3,1,0,2:T(8,128)(2,1)} copy(bf16[23,16,46,256]{3,2,1,0:T(8,128)(2,1)} %get-tuple-element.233) | data formatting | bytes 17334272 | tf_op jit(solution)/shard_map/convert.6
  138.6 11.3 %fusion.48 = bf16[84,2,46,361]{3,1,2,0:T(2,128)(2,1)} fusion(s32[1,84,2,46,361]{4,2,3,1,0:T(2,128)} %param.6, pred[46,361]{1,0:T(8,128)(4,1)S(1)} %iota_compare_fusion), kind=kLoop, calls=%fused_computation.136 | loop fusion | flops 11159232 | bytes 16755454 | tf_op jit(solution)/shard_map/reshape.8
  149.9 6.9 %convert_bitcast_fusion = bf16[1,84,256,2,46]{2,1,3,4,0:T(8,128)(2,1)} fusion(bf16[84,2,46,361]{3,1,2,0:T(2,128)(2,1)} %fusion.48, bf16[368,46,256]{2,0,1:T(8,128)(2,1)S(1)} %bitcast.379), kind=kOutput, calls=%fused_computation.137 | convolution fusion | flops 1430360064 | bytes 18203488 | tf_op jit(solution)/shard_map/ecpml,lmt->ectpm/dot_general | solution.py:118
  156.8 7.8 %copy.41 = bf16[1,84,256,2,46]{1,2,4,3,0:T(8,128)(2,1)} copy(bf16[1,84,256,2,46]{2,1,3,4,0:T(8,128)(2,1)} %convert_bitcast_fusion) | data formatting | bytes 7913472 | tf_op jit(solution)/shard_map/convert_element_type | solution.py:120
  164.7 5.7 %copy.55 = bf16[16,8,1,84,1,1,2,2,46]{3,1,0,8,7,6,5,4,2:T(8,128)(2,1)S(1)} copy(bf16[16,8,1,84,1,1,2,2,46]{3,6,0,1,8,7,5,4,2:T(2,128)(2,1)} %bitcast.377) | data formatting | bytes 7913472 | tf_op jit(solution)/shard_map/transpose;transpose | solution.py:24
  170.4 27.3 %copy.43 = bf16[128,1,84,1,1,2,2,46]{2,6,7,5,4,3,1,0:T(2,128)(2,1)} copy(bf16[128,1,84,1,1,2,2,46]{2,0,7,6,5,4,3,1:T(8,128)(2,1)S(1)} %bitcast.378) | data formatting | bytes 7913472 | tf_op jit(solution)/shard_map/reshape | solution.py:26
  197.7 11.9 %all-to-all-start.1 = ((bf16[128,1,84,1,1,2,2,46]{2,6,7,5,4,3,1,0:T(2,128)(2,1)}), bf16[128,1,84,1,1,2,2,46]{2,6,7,5,4,3,1,0:T(2,128)(2,1)}, u32[]{:S(2)}, u32[]{:S(2)}) async-start(bf16[128,1,84,1,1,2,2,46]{2,6,7,5,4,3,1,0:T(2,128)(2,1)} %copy.43), calls=%async_computation.1 | async-start | bytes 12058624 | tf_op jit(solution)/shard_map/all_to_all | solution.py:27
  209.6 11.3 %copy.36 = bf16[1,84,32,1440]{3,1,2,0:T(8,128)(2,1)} copy(bf16[1,84,32,1440]{3,2,1,0:T(8,128)(2,1)} %param.5) | data formatting | bytes 15482880 | tf_op args[0]
  220.9 12.9 %copy.37 = bf16[1,84,16,2,1440]{4,3,1,0,2:T(2,128)(2,1)} copy(bf16[1,84,16,2,1440]{4,1,3,2,0:T(8,128)(2,1)} %bitcast.375) | data formatting | bytes 15482880 | tf_op jit(solution)/shard_map/reshape | solution.py:126
  233.8 45.8 %all-to-all-done.1 = bf16[128,1,84,1,1,2,2,46]{2,6,7,5,4,3,1,0:T(2,128)(2,1)} async-done(((bf16[128,1,84,1,1,2,2,46]{2,6,7,5,4,3,1,0:T(2,128)(2,1)}), bf16[128,1,84,1,1,2,2,46]{2,6,7,5,4,3,1,0:T(2,128)(2,1)}, u32[]{:S(2)}, u32[]{:S(2)}) %all-to-all-start.1) | async-done | bytes 3956768 | tf_op jit(solution)/shard_map/all_to_all | solution.py:27
  279.6 9.2 %all-to-all-start = ((bf16[1,84,16,2,1440]{4,3,1,0,2:T(2,128)(2,1)}), bf16[1,84,16,2,1440]{4,3,1,0,2:T(2,128)(2,1)}, u32[]{:S(2)}, u32[]{:S(2)}) async-start(bf16[1,84,16,2,1440]{4,3,1,0,2:T(2,128)(2,1)} %copy.37), calls=%async_computation | async-start | bytes 16515072 | tf_op jit(solution)/shard_map/all_to_all | solution.py:133
  288.8 9.8 %multiply_convert_fusion.1 = (bf16[1,368,1440]{2,1,0:T(8,128)(2,1)S(1)}, bf16[1,368,1440]{2,1,0:T(8,128)(2,1)S(1)}) fusion(f32[368]{0:T(512)S(1)} %fusion.58), kind=kLoop, calls=%fused_computation.143 | loop fusion | flops 6888960 | bytes 2121152 | tf_op jit(solution)/shard_map/convert.3
  298.8 24.1 %copy.44 = bf16[16,8,1,84,1,1,2,2,46]{8,1,7,6,3,0,5,4,2:T(8,128)(2,1)} copy(bf16[16,8,1,84,1,1,2,2,46]{3,7,8,6,1,0,5,4,2:T(2,128)(2,1)} %bitcast.18) | data formatting | bytes 7913472 | tf_op jit(solution)/shard_map/reshape | solution.py:28
  322.9 16.2 %reshape_reshape.7 = bf16[2688,736]{1,0:T(8,128)(2,1)} reshape(bf16[16,84,1,1,2,2,8,46]{7,6,5,4,1,0,3,2:T(8,128)(2,1)} %bitcast.373) | data formatting | bytes 7913472 | tf_op jit(solution)/shard_map/reshape;reshape | solution.py:128
  339.1 11.2 %convolution_convert_fusion = bf16[2688,1440]{0,1:T(8,128)(2,1)} fusion(bf16[2688,736]{1,0:T(8,128)(2,1)} %reshape_reshape.7, bf16[736,1440]{1,0:T(8,128)(2,1)S(1)} %bitcast.396), kind=kOutput, calls=%fused_computation.130 | convolution fusion | flops 5701570560 | bytes 13817856 | tf_op jit(solution)/shard_map/dot_general | solution.py:129
  350.3 11.6 %copy.45 = bf16[2688,1440]{1,0:T(8,128)(2,1)} copy(bf16[2688,1440]{0,1:T(8,128)(2,1)} %convolution_convert_fusion) | data formatting | bytes 15482880 | tf_op jit(solution)/shard_map/convert_element_type | solution.py:129
  361.9 17.0 %reshape.1212 = bf16[16,84,1,2,1440]{4,3,1,0,2:T(2,128)(2,1)} reshape(bf16[2688,1440]{1,0:T(8,128)(2,1)} %copy.45) | data formatting | bytes 15482880 | tf_op jit(solution)/shard_map/reshape | solution.py:130
  378.9 9.6 %convert_reduce_fusion = f32[84,2,1440]{2,1,0:T(2,128)S(1)} fusion(bf16[16,84,1,2,1440]{4,3,1,0,2:T(2,128)(2,1)} %reshape.1212), kind=kLoop, calls=%fused_computation.125 | loop fusion | flops 7499520 | bytes 8709120 | tf_op jit(solution)/shard_map/reduce_sum | solution.py:132
  389.0 15.5 %fusion.46 = bf16[16,84,1,2,1440]{4,3,2,1,0:T(2,128)(2,1)S(1)} fusion(f32[84,2,1440]{2,1,0:T(2,128)S(1)} %broadcast_multiply_fusion, bf16[16,84,1,2,1440]{4,3,1,0,2:T(2,128)(2,1)} %reshape.1212, f32[84]{0:T(128)S(1)} %copy-done.1, bf16[1,84,16,2,1440]{4,3,1,0,2:T(2,128)(2,1)} %all-to-all-done), kind=kLoop, calls=%fused_computation.133 | loop fusion | flops 23224320 | bytes 24192336 | tf_op jit(solution)/shard_map/convert_element_type | solution.py:134
  404.5 98.2 %all_to_all.29 = bf16[16,84,1,2,1440]{4,3,2,1,0:T(2,128)(2,1)} all-to-all(bf16[16,84,1,2,1440]{4,3,2,1,0:T(2,128)(2,1)S(1)} %fusion.46), channel_id=1, replica_groups=mesh['member'=16,'space'=8] {'member'}, dimensions={0} | all-to-all | bytes 15482880 | tf_op jit(solution)/shard_map/all_to_all | solution.py:137
  502.7 8.5 %copy.47 = bf16[1,84,16,1,2,1440]{5,1,4,2,3,0:T(8,128)(2,1)} copy(bf16[1,84,16,1,2,1440]{5,4,1,2,3,0:T(2,128)(2,1)} %bitcast.376) | data formatting | bytes 15482880 | tf_op jit(solution)/shard_map/all_to_all | solution.py:137
  511.1 9.5 %copy.48 = bf16[1,84,32,1440]{3,2,1,0:T(8,128)(2,1)} copy(bf16[1,84,32,1440]{3,1,2,0:T(8,128)(2,1)} %bitcast.374) | data formatting | bytes 15482880 | tf_op jit(solution)/shard_map/reshape | solution.py:138
  (1172 shorter events, 82.7 us)
Async XLA Ops:
  138.6 11.3 %copy-start = (bf16[23,16,46,256]{3,1,0,2:T(8,128)(2,1)S(1)}, bf16[23,16,46,256]{3,1,0,2:T(8,128)(2,1)}, u32[]{:S(2)}) copy-start(bf16[23,16,46,256]{3,1,0,2:T(8,128)(2,1)} %copy.39) | copy-start | bytes 26001412
  197.7 81.9 %all-to-all-start.1 = ((bf16[128,1,84,1,1,2,2,46]{2,6,7,5,4,3,1,0:T(2,128)(2,1)}), bf16[128,1,84,1,1,2,2,46]{2,6,7,5,4,3,1,0:T(2,128)(2,1)}, u32[]{:S(2)}, u32[]{:S(2)}) async-start(bf16[128,1,84,1,1,2,2,46]{2,6,7,5,4,3,1,0:T(2,128)(2,1)} %copy.43), calls=%async_computation.1 | async-start | bytes 12058624 | tf_op jit(solution)/shard_map/all_to_all | solution.py:27
  279.6 109.4 %all-to-all-start = ((bf16[1,84,16,2,1440]{4,3,1,0,2:T(2,128)(2,1)}), bf16[1,84,16,2,1440]{4,3,1,0,2:T(2,128)(2,1)}, u32[]{:S(2)}, u32[]{:S(2)}) async-start(bf16[1,84,16,2,1440]{4,3,1,0,2:T(2,128)(2,1)} %copy.37), calls=%async_computation | async-start | bytes 16515072 | tf_op jit(solution)/shard_map/all_to_all | solution.py:133
  378.9 10.1 %copy-start.1 = (f32[84]{0:T(128)S(1)}, f32[84]{0:T(128)}, u32[]{:S(2)}) copy-start(f32[84]{0:T(128)} %param.7) | copy-start | bytes 1012
where the time goes:
time: 530 us; the launch traced here: 521 us
  local copies, waits for them, and re-layouts  195 us (37%)
  other arithmetic  115 us (22%)
  blocking collectives  98.2 us (19%)
  waiting for transfers between devices  45.8 us (9%)
  loops' own time  27.1 us (5%)
  starting transfers between devices  21.1 us (4%)
  matrix products  18.1 us (3%)
    all_to_all x1, blocking collectives, local(): lax.all_to_all(perturbed, 'member', split_axis=0, concat_axis=2, tiled=True)  98.2 us
    while x345, other arithmetic  53.9 us
    all_to_all x1, waiting for transfers between devices, exchange_both(): parts = lax.all_to_all(parts, axis, split_axis=0, concat_axis=0, tiled=True)  45.8 us
    reshape x1, local copies, waits for them, and re-layouts, exchange_both(): parts = parts.reshape(-1, *inside)  27.3 us
    another operation x1, loops' own time, legendre_table(): lax.scan(advance, (empty, empty), jnp.arange(turn_count, dtype=jnp.int32))  27.1 us
    reshape x1, local copies, waits for them, and re-layouts, exchange_both(): parts = joined_along(parts.reshape(*sizes, *inside), concats[0] + 1)  24.1 us
    another operation x5, other arithmetic  21.5 us
    dynamic_update_slice x23, local copies, waits for them, and re-layouts, legendre_table(): lax.scan(advance, (empty, empty), jnp.arange(turn_count, dtype=jnp.int32))  18.2 us
  transfers between devices with their start and end apart: 2, of which 1 were waited for; matrix products, arithmetic and copies ran while one was open for 24% of the time, Pallas kernels for 0%

commit v1 on v0

v1 whole, which is shorter than its diff:
```python
import functools
import math

import jax
import jax.numpy as jnp
from jax import lax
from jax.experimental import pallas as pl
from jax.experimental.pallas import tpu as pltpu
from jax.sharding import PartitionSpec as P

F32 = jnp.float32
BF16 = jnp.bfloat16
SLOTS = 48
LEG_PITCH = 369
UNI_PITCH = 49
LEG_UNROLL = 8
VMEM = 60 * 2**20


def synthesis_kernel(first_ref, table_ref, coef_hbm, out_ref, coef, leg, uni, sem):
    channels, order_local, _, degree_count = coef.shape
    pairs = 2 * channels
    fetch = pltpu.make_async_copy(coef_hbm, coef, sem)
    fetch.start()
    order = lax.broadcasted_iota(jnp.int32, (SLOTS, 128), 0) + first_ref[0]
    order_square = order.astype(F32) * order.astype(F32)
    cosine = [jnp.broadcast_to(table_ref[0:1, 128 * h : 128 * h + 128], (SLOTS, 128)) for h in range(2)]
    diagonal = [table_ref[8 : 8 + SLOTS, 128 * h : 128 * h + 128] for h in range(2)]
    uni[0, 0:SLOTS, :] = jnp.zeros((SLOTS, 128), F32)
    empty = uni[0, 0:SLOTS, :]

    def advance(degree, carry):
        older, newer, down = carry
        value = jnp.full((8, 128), degree, jnp.int32).astype(F32)
        square = value * value
        inverse = 1.0 / (4.0 * square - 1.0)
        square = jnp.concatenate([square] * (SLOTS // 8))
        inverse = jnp.concatenate([inverse] * (SLOTS // 8))
        ratio = jnp.maximum((square - order_square) * inverse, 1e-30)
        up = lax.rsqrt(ratio)
        hit = order == degree
        made = []
        for h in range(2):
            row = jnp.where(hit, diagonal[h], up * (cosine[h] * newer[h] - down * older[h]))
            leg[h, pl.ds(degree, SLOTS, stride=LEG_PITCH), :] = row
            made.append(row)
        return newer, tuple(made), ratio * up

    def advance_some(turn, carry):
        for u in range(LEG_UNROLL):
            carry = advance(turn * LEG_UNROLL + u, carry)
        return carry

    lax.fori_loop(0, -(-degree_count // LEG_UNROLL), advance_some, ((empty, empty), (empty, empty), empty))
    fetch.wait()
    factor = math.sqrt(3.0) * math.sqrt(4.0 * math.pi) / degree_count * 2.0 ** (-30)

    def sum_degrees(m):
        spectral = (coef[:, m, :, :].astype(F32) * factor).reshape(pairs, degree_count).astype(BF16)
        for h in range(2):
            legendre = leg[h, pl.ds(m * LEG_PITCH, degree_count), :].astype(BF16)
            fourier = jnp.dot(spectral, legendre, preferred_element_type=F32)
            uni[h, pl.ds(m, pairs, stride=UNI_PITCH), :] = fourier

    def sum_two(turn, carry):
        sum_degrees(2 * turn)
        sum_degrees(2 * turn + 1)
        return carry

    lax.fori_loop(0, order_local // 2, sum_two, 0)
    blank = jnp.zeros((pairs, 128), F32)
    for h in range(2):
        for m in range(order_local, SLOTS):
            uni[h, pl.ds(m, pairs, stride=UNI_PITCH), :] = blank
    lane_group = lax.broadcasted_iota(jnp.int32, (2 * SLOTS, 128), 1) // 32

    def regroup(q, carry):
        for h in range(2):
            parts = [
                jnp.concatenate([uni[h, pl.ds((8 * q + 2 * i + p) * UNI_PITCH, SLOTS), :] for p in range(2)])
                for i in range(4)
            ]
            for group in range(4):
                joined = None
                for i in range(4):
                    turn = (i - group) % 4
                    moved = parts[i] if turn == 0 else pltpu.roll(parts[i], 32 * turn, 1)
                    joined = moved if joined is None else jnp.where(lane_group == i, moved, joined)
                joined = joined.astype(BF16)
                for j in range(3):
                    t = 3 * q + j
                    row = pl.multiple_of(32 * (t % 4), 32)
                    out_ref[t // 4, 4 * h + group, pl.ds(row, 32), :] = joined[32 * j : 32 * j + 32]
        return carry

    lax.fori_loop(0, channels // 4, regroup, 0)
    for s in range(8):
        out_ref[15, s, 96:128, :] = jnp.zeros((32, 128), BF16)


def centre_kernel(in_ref, out_ref):
    members = in_ref.shape[0]
    total = in_ref[0, 0].astype(F32)
    for e in range(1, members):
        total = total + in_ref[e, 0].astype(F32)
    mean = total * (1.0 / members)
    for e in range(members):
        out_ref[e, 0] = (in_ref[e, 0].astype(F32) - mean).astype(BF16)


def perturb_kernel(groups, scale_ref, rows_ref, basis_ref, weather_ref, out_ref):
    step = pl.program_id(0)
    columns = []
    for g in range(groups):
        pieces = []
        for s in range(8):
            for j in range(3):
                t = 3 * (step * groups + g) + j
                pieces.append(rows_ref[t // 4, s, pl.ds(pl.multiple_of(32 * (t % 4), 32), 32), :])
        columns.append(jnp.concatenate(pieces, axis=0))
    noise = lax.dot_general(
        jnp.concatenate(columns, axis=1), basis_ref[...], (((0,), (0,)), ((), ())), preferred_element_type=F32
    )
    for c in range(4 * groups):
        scale = scale_ref[step * 4 * groups + c]
        out_ref[c] = (weather_ref[c].astype(F32) + scale * noise[32 * c : 32 * c + 32]).astype(BF16)


def legendre_start(first_order, colatitude):
    orders = first_order + jnp.arange(SLOTS, dtype=jnp.int32)
    steps = jnp.arange(1, 384, dtype=jnp.int32)
    terms = 0.5 * jnp.log((2.0 * steps.astype(F32) + 1.0) / (2.0 * steps.astype(F32)))
    logs = jnp.sum(jnp.where(steps[None, :] <= orders[:, None], terms[None, :], 0.0), axis=1)
    diagonal = jnp.exp(
        logs[:, None]
        - 0.5 * math.log(4.0 * math.pi)
        + orders.astype(F32)[:, None] * jnp.log(jnp.sin(colatitude))[None, :]
    )
    cosine = jnp.broadcast_to(jnp.cos(colatitude)[None, :], (8, colatitude.shape[0]))
    return jnp.concatenate([cosine, diagonal])


def fourier_basis(bands, order_local, lon_count):
    slots = jnp.arange(SLOTS, dtype=jnp.int32)
    orders = order_local * jnp.arange(bands, dtype=jnp.int32)[:, None] + slots[None, :]
    columns = jnp.arange(lon_count, dtype=jnp.int32)
    phases = orders[:, :, None] * columns % lon_count
    angles = 2.0 * math.pi / lon_count * phases.astype(F32)
    weights = jnp.where(orders == 0, 1.0, math.sqrt(2.0))
    weights = jnp.where(slots[None, :] < order_local, weights, 0.0).astype(F32)[:, :, None]
    both = jnp.stack([weights * jnp.cos(angles), weights * jnp.sin(angles)], axis=1)
    return both.astype(BF16).reshape(bands * 2 * SLOTS, lon_count)


def local(weather, coefficients, channel_scale):
    members = lax.axis_size("member")
    bands = lax.axis_size("space")
    _, channels, rows_local, lon_count = weather.shape
    order_local, degree_count = coefficients.shape[3:]
    lat_count = rows_local * bands
    first_order = lax.axis_index("space") * order_local
    row_first = (lon_count // 2 + 1 - lat_count) // 2
    colatitude = math.pi * (row_first + jnp.arange(lat_count, dtype=jnp.int32)).astype(F32) / (lon_count // 2)
    vmem = pl.BlockSpec(memory_space=pltpu.VMEM)
    smem = pl.BlockSpec(memory_space=pltpu.SMEM)
    params = pltpu.CompilerParams(vmem_limit_bytes=VMEM)
    block = (members, bands, 128, 128)

    coef = jnp.transpose(coefficients[0], (0, 2, 1, 3))
    fourier = pl.pallas_call(
        synthesis_kernel,
        in_specs=[smem, vmem, pl.BlockSpec(memory_space=pl.ANY)],
        out_specs=vmem,
        out_shape=jax.ShapeDtypeStruct(block, BF16),
        scratch_shapes=[
            pltpu.VMEM((channels, order_local, 2, degree_count), jnp.int32),
            pltpu.VMEM((2, SLOTS * LEG_PITCH + 8, 128), F32),
            pltpu.VMEM((2, 2 * channels * UNI_PITCH, 128), F32),
            pltpu.SemaphoreType.DMA,
        ],
        compiler_params=params,
        name="synthesis",
    )(first_order.reshape(1), legendre_start(first_order, colatitude), coef)

    owned = lax.all_to_all(
        fourier.reshape(members * bands, 128, 128), ("member", "space"), split_axis=0, concat_axis=0, tiled=True
    )
    spec = pl.BlockSpec((members, 1, 128, 128), lambda s: (0, s, 0, 0))
    centred = pl.pallas_call(
        centre_kernel,
        grid=(bands,),
        in_specs=[spec],
        out_specs=spec,
        out_shape=jax.ShapeDtypeStruct(block, BF16),
        compiler_params=params,
        name="centre",
    )(owned.reshape(block))
    rows = lax.all_to_all(centred, "member", split_axis=0, concat_axis=0, tiled=True)

    groups = 7
    band = pl.BlockSpec((4 * groups, rows_local, lon_count), lambda i: (i, 0, 0))
    basis = fourier_basis(bands, order_local, lon_count)
    perturbed = pl.pallas_call(
        functools.partial(perturb_kernel, groups),
        grid=(channels // (4 * groups),),
        in_specs=[
            smem,
            pl.BlockSpec(block, lambda i: (0, 0, 0, 0)),
            pl.BlockSpec(basis.shape, lambda i: (0, 0)),
            band,
        ],
        out_specs=band,
        out_shape=jax.ShapeDtypeStruct(weather.shape[1:], BF16),
        compiler_params=params,
        name="perturb",
    )(channel_scale, rows, basis, weather[0])
    return perturbed[None]


def solution(mesh):
    return jax.shard_map(
        local,
        mesh=mesh,
        in_specs=(P("member", None, "space", None), P("member", None, None, "space", None), P()),
        out_specs=P("member", None, "space", None),
        check_vma=False,
    )
```

time: 530 us -> 162 us (0.31); the launches traced: 521 us -> 162 us
  local copies, waits for them, and re-layouts: 195 us -> 0.01 us
  other arithmetic: 115 us -> 13.5 us
  Pallas kernels: 0 us -> 41.8 us
  blocking collectives: 98.2 us -> 62.5 us
  loops' own time: 27.1 us -> 0 us
  matrix products: 18.1 us -> 0 us
  starting transfers between devices: 21.1 us -> 6.9 us
  waiting for transfers between devices: 45.8 us -> 37.1 us
    reshape x6 -> x0, local copies, waits for them, and re-layouts: 90.9 us -> none  [the longest x1 27.3 us: exchange_both(): parts = parts.reshape(-1, *inside)]
    while x345 -> x0, other arithmetic: 53.9 us -> none
    pallas_call x0 -> x3, Pallas kernels: none -> 41.8 us  [the longest x1 21.8 us: local(): pl.pallas_call(synthesis_kernel, in_specs=[smem, vmem, pl.BlockSpec(memor...]
    all_to_all x1, blocking collectives: 98.2 us -> 62.5 us  [local(): lax.all_to_all(fourier.reshape(members * bands, 128, 128), ('member', 'sp...]
    another operation x4 -> x0, local copies, waits for them, and re-layouts: 32.1 us -> none  [the longest x1 16.2 us: local(): banded.reshape(member_count * channels * lat_local, 2 * order_count)]
    another operation x1 -> x0, loops' own time: 27.1 us -> none  [legendre_table(): lax.scan(advance, (empty, empty), jnp.arange(turn_count, dtype=jnp.int32))]
    convert_element_type x2 -> x0, local copies, waits for them, and re-layouts: 19.5 us -> none  [the longest x1 11.6 us: local(): jnp.dot(fourier_rows, basis, preferred_element_type=jnp.float32)]
    dynamic_update_slice x23 -> x0, local copies, waits for them, and re-layouts: 18.2 us -> none  [legendre_table(): lax.scan(advance, (empty, empty), jnp.arange(turn_count, dtype=jnp.int32))]
  transfers between devices with their start and end apart: 2 -> 1, of which waited for: 1 -> 1; matrix products, arithmetic and copies ran while one was open for 24% -> 8% of each run, Pallas kernels for 0% -> 0%
where the time goes in v1:
time: 162 us
  blocking collectives  62.5 us (39%)
  Pallas kernels  41.8 us (26%)
  waiting for transfers between devices  37.1 us (23%)
  other arithmetic  13.5 us (8%)
  starting transfers between devices  6.9 us (4%)
    all_to_all x1, blocking collectives, local(): lax.all_to_all(fourier.reshape(members * bands, 128, 128), ('member', 'sp...  62.5 us
    all_to_all x1, waiting for transfers between devices, local(): lax.all_to_all(centred, 'member', split_axis=0, concat_axis=0, tiled=True)  37.1 us
    pallas_call x1, Pallas kernels, local(): pl.pallas_call(synthesis_kernel, in_specs=[smem, vmem, pl.BlockSpec(memor...  21.8 us
    pallas_call x1, Pallas kernels, local(): pl.pallas_call(functools.partial(perturb_kernel, groups), grid=(channels...  12.8 us
    another operation x1, other arithmetic  10.7 us
    pallas_call x1, Pallas kernels, local(): pl.pallas_call(centre_kernel, grid=(bands,), in_specs=[spec], out_specs=s...  7.16 us
    all_to_all x1, starting transfers between devices, local(): lax.all_to_all(centred, 'member', split_axis=0, concat_axis=0, tiled=True)  6.9 us
  transfers between devices with their start and end apart: 1, of which 1 were waited for; matrix products, arithmetic and copies ran while one was open for 8% of the time, Pallas kernels for 0%

profile of v1, /device:TPU:1, one launch (start us, length us, event | category | flops | bytes accessed | tf_op | source)
XLA Modules:
  0.0 161.8 jit_solution(4630211379461670045)
XLA Ops:
  0.1 0.2 select_reduce_fusion
  0.3 0.1 add_exponential_fusion
  0.4 0.6 pad_maximum_fusion.1.table_ref
  1.1 21.8 %synthesis.1 = bf16[16,8,128,128]{3,2,1,0:T(8,128)(2,1)} custom-call(s32[1]{0:T(128)} %bitcast.first_ref, f32[56,256]{1,0:T(8,128)} %pad_maximum_fusion.1.table_ref, s32[84,46,2,361]{3,2,1,0:T(2,128)} %bitcast.11), custom_call_target="tpu_custom_call" | custom-call | tf_op jit(solution)/shard_map/synthesis/pallas_call | solution.py:170
  22.9 62.5 %all_to_all.10 = bf16[128,128,128]{2,1,0:T(8,128)(2,1)} all-to-all(bf16[128,128,128]{2,1,0:T(8,128)(2,1)} %bitcast.9), channel_id=1, replica_groups=mesh['member'=16,'space'=8] {'member','space'}, dimensions={0} | all-to-all | bytes 8388608 | tf_op jit(solution)/shard_map/all_to_all | solution.py:185
  85.4 7.2 %centre.1 = bf16[16,8,128,128]{3,2,1,0:T(8,128)(2,1)} custom-call(bf16[16,8,128,128]{3,2,1,0:T(8,128)(2,1)} %bitcast.10), custom_call_target="tpu_custom_call" | custom-call | tf_op jit(solution)/shard_map/centre/pallas_call | solution.py:189
  92.6 6.9 %all-to-all-start.1 = ((bf16[16,8,128,128]{3,2,1,0:T(8,128)(2,1)}), bf16[16,8,128,128]{3,2,1,0:T(8,128)(2,1)}, u32[]{:S(2)}, u32[]{:S(2)}) async-start(bf16[16,8,128,128]{3,2,1,0:T(8,128)(2,1)} %centre.1), calls=%async_computation.1 | async-start | bytes 8388608 | tf_op jit(solution)/shard_map/all_to_all | solution.py:198
  99.5 0.1 iota_add_fusion
  99.5 0.1 select_select_fusion
  99.6 10.7 %multiply_convert_fusion.1 = (bf16[8,1,48,1440]{3,2,1,0:T(8,128)(2,1)S(1)}, bf16[8,1,48,1440]{3,2,1,0:T(8,128)(2,1)S(1)}) fusion(s32[8,48]{1,0:T(8,128)S(1)} %iota_add_fusion, f32[8,48]{1,0:T(8,128)S(1)} %select_select_fusion), kind=kLoop, calls=%fused_computation.5 | loop fusion | flops 7188480 | bytes 2214912 | tf_op jit(solution)/shard_map/convert
  110.3 1.6 %pad_maximum_fusion = bf16[8,2,48,1440]{3,2,1,0:T(8,128)(2,1)} fusion(bf16[8,1,48,1440]{3,2,1,0:T(8,128)(2,1)S(1)} %get-tuple-element.6, bf16[8,1,48,1440]{3,2,1,0:T(8,128)(2,1)S(1)} %get-tuple-element.5), kind=kLoop, calls=%fused_computation.3 | loop fusion | flops 1105920 | bytes 4423680 | tf_op jit(solution)/shard_map/stack | solution.py:151
  112.0 37.1 %all-to-all-done.1.rows_ref = bf16[16,8,128,128]{3,2,1,0:T(8,128)(2,1)} async-done(((bf16[16,8,128,128]{3,2,1,0:T(8,128)(2,1)}), bf16[16,8,128,128]{3,2,1,0:T(8,128)(2,1)}, u32[]{:S(2)}, u32[]{:S(2)}) %all-to-all-start.1) | async-done | bytes 4194336 | tf_op jit(solution)/shard_map/all_to_all | solution.py:198
  149.1 12.8 %perturb.1 = bf16[84,32,1440]{2,1,0:T(8,128)(2,1)} custom-call(f32[84]{0:T(128)} %scale_ref.1, bf16[16,8,128,128]{3,2,1,0:T(8,128)(2,1)} %all-to-all-done.1.rows_ref, bf16[768,1440]{1,0:T(8,128)(2,1)} %bitcast.12, bf16[84,32,1440]{2,1,0:T(8,128)(2,1)} %bitcast.13), custom_call_target="tpu_custom_call" | custom-call | tf_op jit(solution)/shard_map/perturb/pallas_call | solution.py:203
  (9 shorter events, 0.1 us)
Async XLA Ops:
  92.6 56.5 %all-to-all-start.1 = ((bf16[16,8,128,128]{3,2,1,0:T(8,128)(2,1)}), bf16[16,8,128,128]{3,2,1,0:T(8,128)(2,1)}, u32[]{:S(2)}, u32[]{:S(2)}) async-start(bf16[16,8,128,128]{3,2,1,0:T(8,128)(2,1)} %centre.1), calls=%async_computation.1 | async-start | bytes 8388608 | tf_op jit(solution)/shard_map/all_to_all | solution.py:198
